TPU v7x, 128 devices: a whole 4x4x4 slice. The times are simulated.
128 devices in a mesh: shard: 32 (over y, x, core), tp: 4 (over z).
Axes of the slice: x: 4, y: 4, z: 4, core: 2. Of those that a mesh axis runs over, the one named last changes fastest.
Arguments:
- weight_gate: bfloat16 [2560, 9728], P('shard', 'tp'), may hold values from -0.21875 to 0.21875
- low_gate: bfloat16 [2560, 32], P('shard'), may hold values from -0.125 to 0.125
- high_gate: bfloat16 [32, 9728], P(None, 'tp'), may hold values from -1 to 1
- weight_up: bfloat16 [2560, 9728], P('shard', 'tp'), may hold values from -0.21875 to 0.21875
- low_up: bfloat16 [2560, 32], P('shard'), may hold values from -0.125 to 0.125
- high_up: bfloat16 [32, 9728], P(None, 'tp'), may hold values from -1 to 1
- norm_gain: float32 [2560], P('shard'), may hold values from 0.25 to 1.75
Outputs:
- ready_gate: bfloat16 [2560, 9728], P(None, 'tp')
- ready_up: bfloat16 [2560, 9728], P(None, 'tp')
- factor_gate: float32 [9728], P('tp')
- factor_up: float32 [9728], P('tp')
All inputs are finite; a program needn't handle non-finite values.
Results may differ from a plain program's by a relative error of at most 0.001.
Values may be sent and summed in bfloat16 or wider, within the bound.
A program may use at most 128 MiB of HBM per device.

v0:
```python
import jax
import jax.numpy as jnp
from jax import lax
from jax.sharding import PartitionSpec as P

mix_rate = 2.0


def sent_to_all(array, axis):
    size = lax.axis_size(axis)
    return lax.all_to_all(
        jnp.broadcast_to(array[None], (size, *array.shape)), axis, 0, 0, tiled=True
    )


def taken_together(array, axis):
    everything = sent_to_all(array, axis)
    return jnp.sum(everything, axis=0)


def in_one(arrays, axis):
    ends = [0]
    for a in arrays:
        ends.append(ends[-1] + a.size)
    so_far = taken_together(jnp.concatenate([a.ravel() for a in arrays]), axis)
    return tuple((so_far[b:e].reshape(a.shape) for a, b, e in zip(arrays, ends, ends[1:])))


def in_one_piece(arrays, axis, dim, along):
    widths = [a.shape[along] for a in arrays]
    both = jnp.concatenate(arrays, axis=along)
    filled = lax.all_gather(both, axis, axis=dim, tiled=True)
    return tuple(jnp.split(filled, [sum(widths[:k]) for k in range(1, len(widths))], axis=along))


def local(weight_gate, low_gate, high_gate, weight_up, low_up, high_up, norm_gain):
    latest_gate = weight_gate.astype(jnp.float32) + mix_rate * jnp.dot(
        low_gate, high_gate, preferred_element_type=jnp.float32
    )
    latest_up = weight_up.astype(jnp.float32) + mix_rate * jnp.dot(
        low_up, high_up, preferred_element_type=jnp.float32
    )
    latest_gained_gate = latest_gate * norm_gain[:, None]
    latest_gained_up = latest_up * norm_gain[:, None]
    total_gate, total_up = in_one(
        (
            jnp.sum(latest_gained_gate * latest_gained_gate, axis=0),
            jnp.sum(latest_gained_up * latest_gained_up, axis=0),
        ),
        "shard",
    )
    factor_gate = jnp.sqrt(total_gate)
    factor_up = jnp.sqrt(total_up)
    narrow_gate, narrow_up = (
        (latest_gained_gate / factor_gate).astype(jnp.bfloat16),
        (latest_gained_up / factor_up).astype(jnp.bfloat16),
    )
    ready_gate, ready_up = in_one_piece((narrow_gate, narrow_up), "shard", 0, 1)
    return (ready_gate, ready_up, factor_gate, factor_up)


def solution(mesh):
    in_specs = (
        P("shard", "tp"),
        P("shard", None),
        P(None, "tp"),
        P("shard", "tp"),
        P("shard", None),
        P(None, "tp"),
        P("shard"),
    )
    out_specs = (P(None, "tp"), P(None, "tp"), P("tp"), P("tp"))
    return jax.shard_map(local, mesh=mesh, in_specs=in_specs, out_specs=out_specs, check_vma=False)
```

profile of v0, /device:TPU:1, one launch (start us, length us, event | category | flops | bytes accessed | tf_op | source)
XLA Modules:
  0.0 147.7 jit_solution(14768416146276575479)
XLA Ops:
  7.2 0.0 copy-start
  7.2 0.0 all-gather.2.cloned.1.call-start
  7.2 0.9 copy-done
  8.1 1.4 multiply_reduce_fusion.1
  9.5 1.5 multiply_reduce_fusion
  11.0 0.3 broadcast_in_dim.2
  11.3 20.8 %all_to_all.6 = f32[32,1,4864]{2,1,0:T(1,128)S(1)} all-to-all(f32[32,1,4864]{2,1,0:T(1,128)S(1)} %broadcast_in_dim.2), channel_id=1, replica_groups=mesh['shard'=32,'tp'=4] {'shard'}, dimensions={0} | all-to-all | bytes 1245184 | tf_op jit(solution)/shard_map/all_to_all | solution.py:11
  32.1 0.4 reduce_sum.29
  32.5 0.0 copy-start.1
  32.5 0.0 copy-start.2
  32.5 0.1 divide_convert_fusion
  32.7 0.9 pad_maximum_fusion
  33.6 0.0 all-gather.2.cloned.1.call-update
  33.6 90.2 %all-gather.2.cloned.1.call-done = bf16[2560,4864]{1,0:T(8,128)(2,1)} async-done(((bf16[80,4864]{1,0:T(8,128)(2,1)}), bf16[2560,4864]{1,0:T(8,128)(2,1)}) %all-gather.2.cloned.1.call-update) | async-done | bytes 24903696 | tf_op jit(solution)/shard_map/all_gather | solution.py:32
  123.8 17.0 %fusion.4 = (bf16[2560,2432]{1,0:T(8,128)(2,1)}, bf16[2560,2432]{1,0:T(8,128)(2,1)}) fusion(bf16[2560,4864]{1,0:T(8,128)(2,1)} %all-gather.2.cloned.1.call-done), kind=kLoop, calls=%fused_computation.14 | loop fusion | bytes 49807360 | tf_op jit(solution)/shard_map/split | solution.py:33
  140.8 0.0 copy-done.1
  140.8 0.0 copy-done.2
  (2 shorter events, 0.0 us)
Async XLA Ops:
  7.2 0.9 copy-start
  7.2 116.6 %all-gather.2.cloned.1.call-start = ((), (), s32[]{:S(2)}) async-start(), calls=%async_computation.1 | async-start | bytes 25681920 | tf_op jit(solution)/shard_map/all_gather | solution.py:32
  32.5 108.3 %copy-start.1 = (f32[2432]{0:T(1024)}, f32[2432]{0:T(1024)S(1)}, u32[]{:S(2)}) copy-start(f32[2432]{0:T(1024)S(1)} %get-tuple-element.6) | copy-start | bytes 29188
  32.5 108.3 %copy-start.2 = (f32[2432]{0:T(1024)}, f32[2432]{0:T(1024)S(1)}, u32[]{:S(2)}) copy-start(f32[2432]{0:T(1024)S(1)} %get-tuple-element.7) | copy-start | bytes 29188
Sparse Core Ops, SparseCore 0:
  33.8 89.9 all-gather.1
where the time goes:
time: 148 us
  waiting for transfers between devices  90.2 us (61%)
  blocking collectives  20.8 us (14%)
  local copies, waits for them, and re-layouts  18.2 us (12%)
  between operations  14.1 us (10%)
  matrix products  2.84 us (2%)
    all_gather x1, waiting for transfers between devices, in_one_piece(): filled = lax.all_gather(both, axis, axis=dim, tiled=True)  90.2 us
    all_to_all x1, blocking collectives, sent_to_all(): lax.all_to_all(jnp.broadcast_to(array[None], (size, *array.shape)), axis,...  20.8 us
    split x1, local copies, waits for them, and re-layouts, in_one_piece(): jnp.split(filled, [sum(widths[:k]) for k in range(1, len(widths))], axis=...  17 us
  transfers between devices with their start and end apart: 1, of which 1 were waited for; matrix products, arithmetic and copies ran while one was open for 0% of the time, Pallas kernels for 0%

commit v1 on v0

v1 whole, which is shorter than its diff:
```python
import functools

import jax
import jax.numpy as jnp
from jax import lax
from jax.experimental import pallas as pl
from jax.experimental.pallas import tpu as pltpu
from jax.sharding import PartitionSpec as P

MESH = pl.DeviceIdType.MESH
SIDE = 4
BLOCKS = 32
ROWS = 80
HALF = 40
WIDE = 2432
PACK = 128
LINKS = ((0, 1), (0, -1), (1, 1), (1, -1))
ITEMS = 11


def schedule(axis, sign):
    first, second = axis, 1 - axis
    half = 0 if sign == 1 else 1

    def at(along, across):
        return (along, across) if axis == 0 else (across, along)

    return [
        (first, at(0, 0), None),
        (second, at(0, 0), None),
        (first, at(-sign, 0), half),
        (second, at(0, -1), None),
        (second, at(0, 1), None),
        (second, at(-sign, 0), half),
        (second, at(0, 2), half),
        (second, at(0, 2), 1 - half),
        (second, at(-sign, -1), half),
        (second, at(-sign, 1), half),
        (second, at(-sign, 2), half),
    ]


RELEASE = {1: (3, 4, 5), 2: (6,), 3: (7, 8), 4: (9,), 5: (10,), 7: (11,)}


def gather_kernel(
    wg_ref, wu_ref, pk_ref, og_ref, ou_ref,
    own_sem, send_sem, recv_sem, cross_send, cross_recv,
):
    shard = lax.axis_index("shard")
    core = lax.rem(shard, 2)
    chip = shard // 2
    y, x = chip // SIDE, lax.rem(chip, SIDE)
    a = x + core * (y - x)
    b = y + core * (x - y)
    ma, mb = 1 + 3 * core, 4 - 3 * core

    def block(da, db):
        ca = lax.rem(a + da + SIDE, SIDE)
        cb = lax.rem(b + db + SIDE, SIDE)
        return (ca * ma + cb * mb) * 2 + core

    own = block(0, 0)
    partner = own + 1 - 2 * core
    near = [block(sign, 0) if axis == 0 else block(0, sign) for axis, sign in LINKS]

    copies = [
        pltpu.make_async_copy(wg_ref, og_ref.at[own, :, pl.ds(0, WIDE)], own_sem.at[0]),
        pltpu.make_async_copy(pk_ref, og_ref.at[own, :, pl.ds(WIDE, PACK)], own_sem.at[1]),
        pltpu.make_async_copy(wu_ref, ou_ref.at[own], own_sem.at[2]),
    ]
    for c in copies:
        c.start()
    barrier = pltpu.get_barrier_semaphore()
    for other in near + [partner]:
        pl.semaphore_signal(barrier, inc=1, device_id={"shard": other}, device_id_type=MESH)
    pl.semaphore_wait(barrier, 5)
    for c in copies:
        c.wait()

    outs = (og_ref, ou_ref)

    def piece(array, place, half):
        ref = outs[array].at[block(*place)]
        if half is not None:
            ref = ref.at[pl.ds(half * HALF, HALF)]
        return ref

    plans = [schedule(axis, sign) for axis, sign in LINKS]

    def link_copy(link, item):
        array, place, half = plans[link][item]
        ref = piece(array, place, half)
        return pltpu.make_async_remote_copy(
            src_ref=ref, dst_ref=ref,
            send_sem=send_sem.at[link, item], recv_sem=recv_sem.at[link, item],
            device_id={"shard": near[link]}, device_id_type=MESH,
        )

    def arrived(link, item):
        axis, sign = LINKS[link]
        array, (da, db), half = plans[link][item]
        place = (da - sign, db) if axis == 0 else (da, db - sign)
        return array, place, half

    def arrival(link, item):
        ref = piece(*arrived(link, item))
        return pltpu.make_async_remote_copy(
            src_ref=ref, dst_ref=ref,
            send_sem=send_sem.at[link, item], recv_sem=recv_sem.at[link, item],
            device_id={"shard": near[link]}, device_id_type=MESH,
        )

    def cross(slot, ref):
        return pltpu.make_async_remote_copy(
            src_ref=ref, dst_ref=ref,
            send_sem=cross_send.at[slot], recv_sem=cross_recv.at[slot],
            device_id={"shard": partner}, device_id_type=MESH,
        )

    for item in (0, 1):
        for link in range(4):
            link_copy(link, item).start()
    crosses = []

    def hand_over(ref, mirror):
        c = cross(len(crosses), ref)
        c.start()
        crosses.append((c, cross(len(crosses), mirror)))

    def mirror_piece(array, place, half):
        da, db = place
        ca = lax.rem(b + da + SIDE, SIDE)
        cb = lax.rem(a + db + SIDE, SIDE)
        index = (ca * mb + cb * ma) * 2 + 1 - core
        ref = outs[array].at[index]
        if half is not None:
            ref = ref.at[pl.ds(half * HALF, HALF)]
        return ref

    for array in (0, 1):
        hand_over(piece(array, (0, 0), None), mirror_piece(array, (0, 0), None))
    for item in range(ITEMS):
        for link in range(4):
            arrival(link, item).wait_recv()
            hand_over(piece(*arrived(link, item)), mirror_piece(*arrived(link, item)))
        for late in RELEASE.get(item + 1, ()):
            for link in range(4):
                link_copy(link, late - 1).start()
    for item in range(ITEMS):
        for link in range(4):
            link_copy(link, item).wait_send()
    for sent, got in crosses:
        sent.wait_send()
        got.wait_recv()


def gather(wg, wu, pk):
    slots = 2 + 4 * ITEMS
    return pl.pallas_call(
        gather_kernel,
        name="torus_gather",
        out_shape=(
            pltpu.VMEM((BLOCKS, ROWS, WIDE + PACK), jnp.bfloat16),
            pltpu.VMEM((BLOCKS, ROWS, WIDE), jnp.bfloat16),
        ),
        in_specs=[pl.BlockSpec(memory_space=pl.ANY)] * 3,
        out_specs=(pl.BlockSpec(memory_space=pltpu.VMEM),) * 2,
        scratch_shapes=[
            pltpu.SemaphoreType.DMA((3,)),
            pltpu.SemaphoreType.DMA((4, ITEMS)),
            pltpu.SemaphoreType.DMA((4, ITEMS)),
            pltpu.SemaphoreType.DMA((slots,)),
            pltpu.SemaphoreType.DMA((slots,)),
        ],
        compiler_params=pltpu.CompilerParams(
            collective_id=0, has_side_effects=True, vmem_limit_bytes=2 << 20
        ),
    )(wg, wu, pk)


TILE = 256
CHUNK = 160
TOTAL = BLOCKS * ROWS


def finish_kernel(og_ref, ou_ref, hg_ref, hu_ref, rg_ref, ru_ref, fg_ref, fu_ref,
                  gain, gained, out, sem):
    lanes = lax.broadcasted_iota(jnp.int32, (PACK, 128), 0)
    pick = jnp.where((lanes >= 64) & (lanes < 67), 1.0, 0.0).astype(jnp.bfloat16)
    for r in range(0, TOTAL, 320):
        gain[pl.ds(r, 320)] = jnp.dot(
            og_ref[pl.ds(r, 320), pl.ds(WIDE, PACK)], pick, preferred_element_type=jnp.float32
        )
    none = jnp.zeros((32, 128), jnp.bfloat16)

    def halves(parts):
        rhs, refs = [], []
        for array, at in parts:
            at = pl.ds(at, 128)
            if array == 0:
                rhs.append(jnp.concatenate([hg_ref[:, at], none], axis=0))
                refs.append(og_ref.at[:, at])
            else:
                rhs.append(jnp.concatenate([none, hu_ref[:, at]], axis=0))
                refs.append(ou_ref.at[:, at])
        return jnp.concatenate(rhs, axis=1), refs

    def write(slot, parts):
        for half, (array, at) in enumerate(parts):
            dst = (rg_ref, ru_ref)[array].at[:, pl.ds(at, 128)]
            yield pltpu.make_async_copy(out.at[slot, half], dst, sem.at[slot, half])

    def tile(slot, parts):
        rhs, refs = halves(parts)
        acc = jnp.zeros((8, TILE), jnp.float32)
        for r in range(0, TOTAL, CHUNK):
            rows = pl.ds(r, CHUNK)
            d = jnp.dot(og_ref[rows, pl.ds(WIDE, 64)], rhs, preferred_element_type=jnp.float32)
            w = jnp.concatenate([ref[rows].astype(jnp.float32) for ref in refs], axis=1)
            g = gain[rows]
            v = (w + d) * jnp.concatenate([g, g], axis=1)
            gained[rows] = v
            acc = acc + jnp.sum((v * v).reshape(CHUNK // 8, 8, TILE), axis=0)
        total = jnp.sum(acc, axis=0, keepdims=True)
        factor = jnp.sqrt(total)
        inverse = 1.0 / factor
        for half, (array, at) in enumerate(parts):
            (fg_ref, fu_ref)[array][:, pl.ds(at, 128)] = factor[:, half * 128:half * 128 + 128]
        for r in range(0, TOTAL, CHUNK):
            rows = pl.ds(r, CHUNK)
            v = (gained[rows] * inverse).astype(jnp.bfloat16)
            out[slot, 0, rows] = v[:, :128]
            out[slot, 1, rows] = v[:, 128:]
        for c in write(slot, parts):
            c.start()

    def gate_parts(t):
        at = pl.multiple_of(t * TILE, TILE)
        return ((0, at), (0, at + 128))

    def up_parts(t):
        at = pl.multiple_of(t * TILE + 128, 128)
        return ((1, at), (1, pl.multiple_of(at + 128, 128)))

    def wait(slot, parts):
        for c in write(slot, parts):
            c.wait()

    def gate_step(t, carry):
        slot = lax.rem(t, 2)

        @pl.when(t >= 2)
        def _():
            wait(slot, gate_parts(t - 2))

        tile(slot, gate_parts(t))
        return carry

    lax.fori_loop(0, 9, gate_step, 0)
    middle = ((0, 9 * TILE), (1, 0))
    wait(1, gate_parts(7))
    tile(1, middle)

    def up_step(t, carry):
        slot = lax.rem(t, 2)

        @pl.when(t == 0)
        def _():
            wait(0, gate_parts(8))

        @pl.when(t == 1)
        def _():
            wait(1, middle)

        @pl.when(t >= 2)
        def _():
            wait(slot, up_parts(t - 2))

        tile(slot, up_parts(t))
        return carry

    lax.fori_loop(0, 9, up_step, 0)
    wait(1, up_parts(7))
    wait(0, up_parts(8))


def finish(og, ou, hg, hu):
    return pl.pallas_call(
        finish_kernel,
        name="merge_and_scale",
        out_shape=(
            jax.ShapeDtypeStruct((TOTAL, WIDE), jnp.bfloat16),
            jax.ShapeDtypeStruct((TOTAL, WIDE), jnp.bfloat16),
            jax.ShapeDtypeStruct((1, WIDE), jnp.float32),
            jax.ShapeDtypeStruct((1, WIDE), jnp.float32),
        ),
        in_specs=[pl.BlockSpec(memory_space=pltpu.VMEM)] * 4,
        out_specs=(
            pl.BlockSpec(memory_space=pl.ANY),
            pl.BlockSpec(memory_space=pl.ANY),
            pl.BlockSpec(memory_space=pltpu.VMEM),
            pl.BlockSpec(memory_space=pltpu.VMEM),
        ),
        scratch_shapes=[
            pltpu.VMEM((TOTAL, 128), jnp.float32),
            pltpu.VMEM((TOTAL, TILE), jnp.float32),
            pltpu.VMEM((2, 2, TOTAL, 128), jnp.bfloat16),
            pltpu.SemaphoreType.DMA((2, 2)),
        ],
        compiler_params=pltpu.CompilerParams(vmem_limit_bytes=16 << 20),
    )(og, ou, hg, hu)


def packed(low_gate, low_up, gain):
    def cut(v):
        return lax.reduce_precision(v, 8, 7)

    high = cut(gain)
    mid = cut(gain - high)
    low = gain - high - mid
    parts = [2.0 * low_gate.astype(jnp.float32), 2.0 * low_up.astype(jnp.float32)]
    parts += [v[:, None] for v in (high, mid, low)]
    parts.append(jnp.zeros((ROWS, PACK - 67), jnp.float32))
    return jnp.concatenate(parts, axis=1).astype(jnp.bfloat16)


def local(weight_gate, low_gate, high_gate, weight_up, low_up, high_up, norm_gain):
    pk = packed(low_gate, low_up, norm_gain)
    og, ou = gather(weight_gate, weight_up, pk)
    ready_gate, ready_up, factor_gate, factor_up = finish(
        og.reshape(TOTAL, WIDE + PACK), ou.reshape(TOTAL, WIDE), high_gate, high_up
    )
    return ready_gate, ready_up, factor_gate.reshape(WIDE), factor_up.reshape(WIDE)


def solution(mesh):
    in_specs = (
        P("shard", "tp"),
        P("shard", None),
        P(None, "tp"),
        P("shard", "tp"),
        P("shard", None),
        P(None, "tp"),
        P("shard"),
    )
    out_specs = (P(None, "tp"), P(None, "tp"), P("tp"), P("tp"))
    return jax.shard_map(local, mesh=mesh, in_specs=in_specs, out_specs=out_specs, check_vma=False)
```

time: 148 us -> 104 us (0.70)
  Pallas kernels: 0 us -> 95.2 us
  waiting for transfers between devices: 90.2 us -> 0 us
  blocking collectives: 20.8 us -> 0 us
  between operations: 14.1 us -> 0.69 us
  local copies, waits for them, and re-layouts: 18.2 us -> 5.86 us
  matrix products: 2.84 us -> 0 us
    pallas_call x0 -> x2, Pallas kernels: none -> 95.2 us  [the longest x1 75.5 us: gather(): pl.pallas_call(gather_kernel, name='torus_gather', out_shape=(pltpu.VMEM(...]
    all_gather x1 -> x0, waiting for transfers between devices: 90.2 us -> none  [in_one_piece(): filled = lax.all_gather(both, axis, axis=dim, tiled=True)]
    all_to_all x1 -> x0, blocking collectives: 20.8 us -> none  [sent_to_all(): lax.all_to_all(jnp.broadcast_to(array[None], (size, *array.shape)), axis,...]
    split x1 -> x0, local copies, waits for them, and re-layouts: 17 us -> none  [in_one_piece(): jnp.split(filled, [sum(widths[:k]) for k in range(1, len(widths))], axis=...]
    unnamed x6 -> x8, local copies, waits for them, and re-layouts: 0.88 us -> 3.8 us
    dot_general x2 -> x0, matrix products: 2.84 us -> none  [the longest x1 1.46 us: local(): jnp.dot(low_up, high_up, preferred_element_type=jnp.float32)]
    convert_element_type x0 -> x2, local copies, waits for them, and re-layouts: none -> 1.57 us  [the longest x1 0.79 us: packed(): low_gate.astype(jnp.float32)]
  transfers between devices with their start and end apart: 1 -> 0, of which waited for: 1 -> 0; matrix products, arithmetic and copies ran while one was open for 0% -> 0% of each run, Pallas kernels for 0% -> 0%
where the time goes in v1:
time: 104 us
  Pallas kernels  95.2 us (92%)
  local copies, waits for them, and re-layouts  5.86 us (6%)
  other arithmetic  1.93 us (2%)
    pallas_call x1, Pallas kernels, gather(): pl.pallas_call(gather_kernel, name='torus_gather', out_shape=(pltpu.VMEM(...  75.5 us
    pallas_call x1, Pallas kernels, finish(): pl.pallas_call(finish_kernel, name='merge_and_scale', out_shape=(jax.Shap...  19.7 us
    unnamed x8, local copies, waits for them, and re-layouts  3.8 us

profile of v1, /device:TPU:1, one launch (start us, length us, event | category | flops | bytes accessed | tf_op | source)
XLA Modules:
  0.0 103.7 jit_solution(2790652073048334055)
XLA Ops:
  0.6 0.7 fusion.3
  1.3 0.1 copy.20
  1.4 0.1 copy.19
  1.5 0.1 copy.18
  1.7 0.8 copy.16
  2.4 0.8 copy.17
  3.3 0.1 concatenate.4.pk_ref
  3.4 0.0 copy-start
  3.4 1.0 copy-done
  4.4 0.0 copy-start.1
  4.4 1.0 copy-done.1
  5.4 75.5 %torus_gather.1 = (bf16[32,80,2560]{2,1,0:T(8,128)(2,1)S(1)}, bf16[32,80,2432]{2,1,0:T(8,128)(2,1)S(1)}) custom-call(bf16[80,2432]{1,0:T(8,128)(2,1)S(1)} %copy-done, bf16[80,2432]{1,0:T(8,128)(2,1)S(1)} %copy-done.1, bf16[80,128]{1,0:T(8,128)(2,1)S(1)} %concatenate.4.pk_ref), custom_call_target="tpu_custom_call" | custom-call | tf_op jit(solution)/shard_map/torus_gather/pallas_call | solution.py:160
  80.9 0.0 copy-start.2
  80.9 0.9 copy-done.2
  81.8 0.0 copy-start.3
  81.8 0.9 copy-done.3
  82.7 19.7 %merge_and_scale.1 = (bf16[2560,2432]{1,0:T(8,128)(2,1)}, bf16[2560,2432]{1,0:T(8,128)(2,1)}, f32[1,2432]{1,0:T(1,128)S(1)}, f32[1,2432]{1,0:T(1,128)S(1)}) custom-call(bf16[2560,2560]{1,0:T(8,128)(2,1)S(1)} %bitcast.8, bf16[2560,2432]{1,0:T(8,128)(2,1)S(1)} %bitcast.9, bf16[32,2432]{1,0:T(8,128)(2,1)S(1)} %copy-done.2, bf16[32,2432]{1,0:T(8,128)(2,1)S(1)} %copy-done.3), custom_call_target="tpu_custom_call" | custom-call | tf_op jit(solution)/shard_map/merge_and_scale/pallas_call | solution.py:289
  102.4 0.6 reduce
  103.0 0.6 reduce.1
  (2 shorter events, 0.0 us)
Async XLA Ops:
  3.4 1.0 copy-start
  4.4 1.0 copy-start.1
  80.9 0.9 copy-start.2
  81.8 0.9 copy-start.3
